TPU v7x, 8 devices: a whole 2x2x1 slice. The times are simulated.
8 devices in a mesh: data: 2 (over z, y), seq: 4 (over x, core).
Axes of the slice: x: 2, y: 2, z: 1, core: 2. Of those that a mesh axis runs over, the one named last changes fastest.
Arguments:
- tokens: bfloat16 [8, 1024, 384], P('data', 'seq'), parts along dimension 0
- lengths: int32 [8], P('data'), parts along dimension 0
- slot_param: bfloat16 [384, 4096], replicated
- logit_scale: float32 [], replicated
- w_in: bfloat16 [256, 384, 1536], P('seq')
- w_out: bfloat16 [256, 1536, 384], P('seq')
Outputs:
- output: bfloat16 [8, 1024, 384], P('data', 'seq'), parts along dimension 0
There are 2 independent parts. A program takes and returns all parts, laid end to end along the dimension named above; an argument that names none is the same for every part.
All inputs are finite; a program needn't handle non-finite values.
Results may differ from a plain program's by a relative error of at most 0.0138026.
Values are sent between devices in bfloat16 or wider.
A program may use at most 1 GiB of HBM per device.

v0:
```python
import jax
import jax.numpy as jnp
from jax import lax
from jax.sharding import PartitionSpec as P

EPSILON = 1e-6
NEG_FILL = -1e30


def l2_normed(values, axis_dim):
    v32 = values.astype(jnp.float32)
    return (v32 * lax.rsqrt(jnp.sum(v32 * v32, axis=axis_dim, keepdims=True) + EPSILON)).astype(jnp.bfloat16)


def solution(mesh):
    seq_size = mesh.shape["seq"]

    def local_layer(tok_blk, len_blk, slot_param, logit_scale, w_in, w_out):
        batch_loc, tok_loc, d_model = tok_blk.shape
        n_slots = slot_param.shape[1]
        exp_loc = w_in.shape[0]
        slot_loc = n_slots // seq_size
        per_exp = slot_loc // exp_loc
        positions = lax.axis_index("seq") * tok_loc + jnp.arange(tok_loc, dtype=jnp.int32)
        tok_valid = (positions[None, :] < len_blk[:, None])[:, :, None]
        logits = logit_scale * jnp.einsum("btd,dn->btn", l2_normed(tok_blk, 2), l2_normed(slot_param, 0), preferred_element_type=jnp.float32)
        masked = jnp.where(tok_valid, logits, NEG_FILL)
        col_max = lax.pmax(jnp.max(masked, axis=1, keepdims=True), "seq")
        disp_w = jnp.exp(masked - col_max)
        col_sum = lax.psum_scatter(jnp.sum(disp_w, axis=1), "seq", scatter_dimension=1, tiled=True)
        part_sum = jnp.einsum("btn,btd->bnd", disp_w.astype(jnp.bfloat16), tok_blk, preferred_element_type=jnp.float32)
        slot_sum = lax.psum_scatter(part_sum.astype(jnp.bfloat16), "seq", scatter_dimension=1, tiled=True)
        slot_in = (slot_sum.astype(jnp.float32) / col_sum[:, :, None]).astype(jnp.bfloat16)
        slot_grp = slot_in.reshape(batch_loc, exp_loc, per_exp, d_model)
        hidden = jax.nn.gelu(jnp.einsum("besd,edf->besf", slot_grp, w_in, preferred_element_type=jnp.float32)).astype(jnp.bfloat16)
        own_out = jnp.einsum("besf,efd->besd", hidden, w_out, preferred_element_type=jnp.float32).astype(jnp.bfloat16)
        slot_out = lax.all_gather(own_out.reshape(batch_loc, slot_loc, d_model), "seq", axis=1, tiled=True)
        comb_w = jnp.exp(logits - jnp.max(logits, axis=2, keepdims=True))
        row_sum = jnp.sum(comb_w, axis=2, keepdims=True)
        tok_mixed = jnp.einsum("btn,bnd->btd", comb_w.astype(jnp.bfloat16), slot_out, preferred_element_type=jnp.float32) / row_sum
        return jnp.where(tok_valid, tok_mixed, 0.0).astype(jnp.bfloat16)

    return jax.shard_map(local_layer, mesh=mesh, in_specs=(P("data", "seq", None), P("data"), P(None, None), P(), P("seq", None, None), P("seq", None, None)), out_specs=P("data", "seq", None), check_vma=False)
```

profile of v0, /device:TPU:0, one launch (start us, length us, event | category | flops | bytes accessed | tf_op | source)
XLA Modules:
  0.0 352.8 jit_solution(15540824367341357896)
XLA Ops:
  6.5 0.0 all-reduce.2.cloned.1.call-start
  7.2 1.4 fusion.43
  8.6 2.6 fusion.29
  11.2 0.7 broadcast_compare_fusion
  11.9 6.9 %multiply_reduce_fusion = (f32[4,256]{1,0:T(4,128)S(1)}, f32[4,256,4096]{2,1,0:T(8,128)S(1)}) fusion(f32[]{:T(128)S(6)} %copy.29, bf16[384,4096]{1,0:T(8,128)(2,1)} %param.8, f32[4096]{0:T(1024)S(1)} %add_rsqrt_fusion, bf16[4,256,384]{2,1,0:T(8,128)(2,1)} %param.6, f32[4,256]{1,0:T(4,128)S(1)} %add_rsqrt_fusion.1), kind=kOutput, calls=%fused_computation.20 | convolution fusion | flops 3235511296 | bytes 20733956 | tf_op jit(solution)/shard_map/btd,dn->btn/dot_general | solution.py:26
  18.8 0.0 copy-start
  18.8 5.7 %copy-done = f32[4,256,4096]{2,1,0:T(8,128)} copy-done((f32[4,256,4096]{2,1,0:T(8,128)}, f32[4,256,4096]{2,1,0:T(8,128)S(1)}, u32[]{:S(2)}) %copy-start) | copy-done | bytes 16777240
  24.5 0.0 copy-start.1
  24.5 5.3 %fusion.14 = (f32[4,256]{1,0:T(4,128)S(1)}, f32[4,4096]{1,0:T(4,128)}) fusion(f32[4,256,4096]{2,1,0:T(8,128)S(1)} %get-tuple-element.8, f32[4,256]{1,0:T(4,128)S(1)} %get-tuple-element.7, f32[]{:T(128)S(6)} %copy.29, pred[4,256]{1,0:T(4,128)(4,1)S(1)} %broadcast_compare_fusion), kind=kLoop, calls=%fused_computation.16 | loop fusion | flops 20954112 | bytes 16851972 | tf_op jit(solution)/shard_map/reduce_sum | solution.py:39
  29.8 0.0 all-reduce.2.cloned.1.call-update
  29.8 0.0 reduce-scatter.7.cloned.1.call-start
  29.8 28.9 %all-reduce.2.cloned.1.call-done = f32[4,4096]{1,0:T(4,128)} async-done(((f32[4,4096]{1,0:T(4,128)}), f32[4,4096]{1,0:T(4,128)}) %all-reduce.2.cloned.1.call-update) | async-done | bytes 65552 | tf_op jit(solution)/shard_map/pmax | solution.py:28
  58.7 0.0 copy-start.2
  58.7 8.8 %fusion.16 = f32[4,4096]{1,0:T(4,128)S(1)} fusion(f32[4,256,4096]{2,1,0:T(8,128)} %copy-done, f32[4,4096]{1,0:T(4,128)} %all-reduce.2.cloned.1.call-done, f32[]{:T(128)S(6)} %copy.29, pred[4,256]{1,0:T(4,128)(4,1)S(1)} %broadcast_compare_fusion), kind=kLoop, calls=%fused_computation.18 | loop fusion | flops 16760832 | bytes 16909316 | tf_op jit(solution)/shard_map/reduce_sum | solution.py:30
  67.5 2.0 copy.18
  69.4 0.0 reduce-scatter.7.cloned.1.call-update
  69.5 0.0 reduce-scatter.5.cloned.1.call-start
  69.5 0.0 copy-done.1
  69.5 0.0 copy-done.2
  69.5 12.5 %convolution_convert_fusion = bf16[4,4096,384]{2,1,0:T(8,128)(2,1)} fusion(bf16[4,256,384]{2,1,0:T(8,128)(2,1)S(1)} %copy-done.1, f32[4,256,4096]{2,1,0:T(8,128)} %copy-done, f32[4,4096]{1,0:T(4,128)S(1)} %copy-done.2, f32[]{:T(128)S(6)} %copy.29, pred[4,256]{1,0:T(4,128)(4,1)S(1)} %broadcast_compare_fusion), kind=kOutput, calls=%fused_computation.21 | convolution fusion | flops 3244294144 | bytes 30213124 | tf_op jit(solution)/shard_map/btn,btd->bnd/dot_general | solution.py:31
  82.1 0.0 reduce-scatter.5.cloned.1.call-update
  82.1 0.2 all-gather.2.cloned.1.call-start
  82.3 12.8 %reduce-scatter.7.cloned.1.call-done = f32[1024,4]{1,0:T(8,128)} async-done(((f32[4096,4]{1,0:T(8,128)}), f32[1024,4]{1,0:T(8,128)}) %reduce-scatter.7.cloned.1.call-update) | async-done | bytes 16400
  95.1 1.2 copy.19
  96.3 91.9 %reduce-scatter.5.cloned.1.call-done = bf16[4,1024,384]{2,1,0:T(8,128)(2,1)} async-done(((bf16[4,4096,384]{2,1,0:T(8,128)(2,1)}), bf16[4,1024,384]{2,1,0:T(8,128)(2,1)}) %reduce-scatter.5.cloned.1.call-update) | async-done | bytes 3145744 | tf_op jit(solution)/shard_map/reduce_scatter | solution.py:32
  188.3 2.4 divide_convert_fusion
  190.7 31.0 %fusion.11.clone.6 = bf16[4,64,16,1536]{3,2,0,1:T(8,128)(2,1)} fusion(bf16[64,384,1536]{2,1,0:T(8,128)(2,1)} %param.10, bf16[4,64,16,384]{3,2,1,0:T(8,128)(2,1)S(1)} %bitcast.48), kind=kOutput, calls=%fused_computation.12.clone.clone.clone.clone.clone.1 | convolution fusion | flops 4888461312 | bytes 91226112 | tf_op jit(solution)/shard_map/besd,edf->besf/dot_general | solution.py:35
  221.6 29.6 %convert_bitcast_fusion = bf16[4,64,16,384]{3,2,0,1:T(8,128)(2,1)S(1)} fusion(bf16[64,1536,384]{2,1,0:T(8,128)(2,1)} %param.11, bf16[4,64,16,1536]{3,2,0,1:T(8,128)(2,1)} %fusion.11.clone.6), kind=kOutput, calls=%fused_computation.37 | convolution fusion | flops 4833411072 | bytes 91226112 | tf_op jit(solution)/shard_map/besf,efd->besd/dot_general | solution.py:36
  251.3 2.0 copy.14
  253.3 0.0 all-gather.2.cloned.1.call-update
  253.3 80.1 %all-gather.2.cloned.1.call-done = bf16[4,4096,384]{2,1,0:T(8,128)(2,1)} async-done(((bf16[4,1024,384]{2,1,0:T(8,128)(2,1)}), bf16[4,4096,384]{2,1,0:T(8,128)(2,1)}) %all-gather.2.cloned.1.call-update) | async-done | bytes 12582928 | tf_op jit(solution)/shard_map/all_gather | solution.py:37
  333.4 12.9 %select_convert_fusion = bf16[4,256,384]{2,1,0:T(8,128)(2,1)} fusion(bf16[4,4096,384]{2,1,0:T(8,128)(2,1)} %all-gather.2.cloned.1.call-done, f32[4,256,4096]{2,1,0:T(8,128)} %copy-done, f32[4,256]{1,0:T(4,128)S(1)} %get-tuple-element.7, f32[]{:T(128)S(6)} %copy.29, f32[4,256]{1,0:T(4,128)S(1)} %get-tuple-element.5, pred[4,256]{1,0:T(4,128)(4,1)S(1)} %broadcast_compare_fusion), kind=kOutput, calls=%fused_computation.43 | convolution fusion | flops 3234988032 | bytes 30155780 | tf_op jit(solution)/shard_map/btn,bnd->btd/dot_general | solution.py:40
  (3 shorter events, 0.0 us)
Async XLA Ops:
  6.5 52.2 %all-reduce.2.cloned.1.call-start = ((), (), s32[]{:S(2)}) async-start(), calls=%async_computation.2 | async-start | bytes 131072 | tf_op jit(solution)/shard_map/pmax | solution.py:28
  18.8 5.7 %copy-start = (f32[4,256,4096]{2,1,0:T(8,128)}, f32[4,256,4096]{2,1,0:T(8,128)S(1)}, u32[]{:S(2)}) copy-start(f32[4,256,4096]{2,1,0:T(8,128)S(1)} %get-tuple-element.8) | copy-start | bytes 50331652
  24.5 45.0 %copy-start.1 = (bf16[4,256,384]{2,1,0:T(8,128)(2,1)S(1)}, bf16[4,256,384]{2,1,0:T(8,128)(2,1)}, u32[]{:S(2)}) copy-start(bf16[4,256,384]{2,1,0:T(8,128)(2,1)} %param.6) | copy-start | bytes 2359300
  29.8 65.3 %reduce-scatter.7.cloned.1.call-start = ((), (), s32[]{:S(2)}) async-start(), calls=%async_computation.5 | async-start | bytes 2621440
  58.7 10.8 %copy-start.2 = (f32[4,4096]{1,0:T(4,128)S(1)}, f32[4,4096]{1,0:T(4,128)}, u32[]{:S(2)}) copy-start(f32[4,4096]{1,0:T(4,128)} %all-reduce.2.cloned.1.call-done) | copy-start | bytes 196612
  69.5 118.8 %reduce-scatter.5.cloned.1.call-start = ((), (), s32[]{:S(2)}) async-start(), calls=%async_computation.3 | async-start | bytes 15728640 | tf_op jit(solution)/shard_map/reduce_scatter | solution.py:32
  82.1 251.3 %all-gather.2.cloned.1.call-start = ((), (), s32[]{:S(2)}) async-start(), calls=%async_computation.4 | async-start | bytes 15728640 | tf_op jit(solution)/shard_map/all_gather | solution.py:37
Sparse Core Ops, SparseCore 0:
  29.9 28.7 all-reduce.1
  69.6 25.4 reduce-scatter.6
  97.7 90.5 reduce-scatter.4
  253.4 79.9 all-gather.1
where the time goes:
time: 353 us
  waiting for transfers between devices  214 us (61%)
  matrix products  92.9 us (26%)
  other arithmetic  21.1 us (6%)
  between operations  13.9 us (4%)
  local copies, waits for them, and re-layouts  10.9 us (3%)
    reduce_scatter x1, waiting for transfers between devices, local_layer(): lax.psum_scatter(part_sum.astype(jnp.bfloat16), 'seq', scatter_dimension=...  91.9 us
    all_gather x1, waiting for transfers between devices, local_layer(): lax.all_gather(own_out.reshape(batch_loc, slot_loc, d_model), 'seq', axis...  80.1 us
    dot_general x1, matrix products, local_layer(): jnp.einsum('besd,edf->besf', slot_grp, w_in, preferred_element_type=jnp.f...  31 us
    dot_general x1, matrix products, local_layer(): jnp.einsum('besf,efd->besd', hidden, w_out, preferred_element_type=jnp.fl...  29.6 us
    pmax x1, waiting for transfers between devices, local_layer(): col_max = lax.pmax(jnp.max(masked, axis=1, keepdims=True), 'seq')  28.9 us
    dot_general x1, matrix products, local_layer(): jnp.einsum('btn,bnd->btd', comb_w.astype(jnp.bfloat16), slot_out, preferr...  12.9 us
    unnamed x5, waiting for transfers between devices  12.9 us
    dot_general x1, matrix products, local_layer(): jnp.einsum('btn,btd->bnd', disp_w.astype(jnp.bfloat16), tok_blk, preferre...  12.5 us
  transfers between devices with their start and end apart: 4, of which 4 were waited for; matrix products, arithmetic and copies ran while one was open for 4% of the time, Pallas kernels for 0%

commit v1 on v0

v1 whole, which is shorter than its diff:
```python
import functools
import math

import jax
import jax.numpy as jnp
from jax import lax
from jax.experimental import pallas as pl
from jax.experimental.pallas import tpu as pltpu
from jax.sharding import PartitionSpec as P

EPSILON = 1e-6
NEG_FILL = -1e30
LOG2E = 1.0 / math.log(2.0)
F32 = jnp.float32
BF16 = jnp.bfloat16
RING = 7


def unit_rows(v32):
    return (v32 * lax.rsqrt(jnp.sum(v32 * v32, axis=1, keepdims=True) + EPSILON)).astype(BF16)


def gelu_tanh(h):
    inner = h * (math.sqrt(2.0 / math.pi) + (math.sqrt(2.0 / math.pi) * 0.044715) * (h * h))
    half = 0.5 * h
    return half + half * jnp.tanh(inner)


def row_of(col, rows):
    return jnp.broadcast_to(col, (rows, 128)).T[0:1, :]


def layer_kernel(
    scale_ref, len_ref, x_ref, phi_hbm, w1_hbm, w2_hbm, out_ref,
    xg, rm, qrow, pnt, ct, xs, d2r, hr, f1r, f2r, w1b, w2b,
    phi_sem, w1_sem, w2_sem,
    sx_sem, sy_sem, sp_sem, sf_sem, r0_sem, r1_sem,
    rms_sem, rm0_sem, rm1_sem,
    d2s_sem, d2r_sem, hs_sem, hr_sem, f1s_sem, f1r_sem, f2s_sem, f2r_sem,
):
    nb, tok, dm = x_ref.shape
    slots = pnt.shape[0]
    n_slots = phi_hbm.shape[1]
    n_exp = slots // 16
    d = lax.axis_index("data")
    s = lax.axis_index("seq")
    xc, core = s // 2, s % 2
    to_p = {"data": d, "seq": 2 * xc + (1 - core)}
    to_x = {"data": d, "seq": 2 * (1 - xc) + core}
    to_y = {"data": 1 - d, "seq": s}

    def remote(src, dst, send, recv, dev):
        return pltpu.make_async_remote_copy(src_ref=src, dst_ref=dst, send_sem=send, recv_sem=recv, device_id=dev, device_id_type=pl.DeviceIdType.MESH)

    def weight_copies(e, slot):
        return (
            pltpu.make_async_copy(w1_hbm.at[n_exp * d + e], w1b.at[slot], w1_sem.at[slot]),
            pltpu.make_async_copy(w2_hbm.at[n_exp * d + e], w2b.at[slot], w2_sem.at[slot]),
        )

    barrier = pltpu.get_barrier_semaphore()
    for dev in (to_p, to_x, to_y):
        pl.semaphore_signal(barrier, inc=1, device_id=dev, device_id_type=pl.DeviceIdType.MESH)

    def send_x(b):
        return remote(x_ref.at[b], xg.at[1, b, 0], sx_sem.at[b], r0_sem.at[4 + b], to_x)

    def send_y(b):
        return remote(x_ref.at[b], xg.at[2, b, 0], sy_sem.at[b], r0_sem.at[8 + b], to_y)

    def send_p(b):
        return remote(x_ref.at[b], xg.at[0, b, 1], sp_sem.at[b], r1_sem.at[b], to_p)

    def fwd_p(r, b):
        return remote(xg.at[r, b, 0], xg.at[r, b, 1], sp_sem.at[4 * r + b], r1_sem.at[4 * r + b], to_p)

    def fwd_y(b):
        return remote(xg.at[1, b, 0], xg.at[3, b, 0], sf_sem.at[b], r0_sem.at[12 + b], to_y)

    def fwd_x(b):
        return remote(xg.at[2, b, 0], xg.at[3, b, 0], sf_sem.at[b], r0_sem.at[12 + b], to_x)

    rm_x = remote(rm.at[0, 0], rm.at[1, 0], rms_sem.at[0], rm0_sem.at[1], to_x)
    rm_y = remote(rm.at[0, 0], rm.at[2, 0], rms_sem.at[1], rm0_sem.at[2], to_y)
    rm_f = remote(rm.at[1, 0], rm.at[3, 0], rms_sem.at[2], rm0_sem.at[3], to_y)
    rm_p = [remote(rm.at[r, 0], rm.at[r, 1], rms_sem.at[3 + r], rm1_sem.at[r], to_p) for r in range(4)]

    def phase_dispatch(phi, acc, m_s, z_s):
        phi_copy = pltpu.make_async_copy(phi_hbm, phi, phi_sem.at[0])
        phi_copy.start()
        pl.semaphore_wait(barrier, 3)
        for b in range(nb):
            send_x(b).start()
            send_y(b ^ 1).start()
        for b in range(nb):
            send_p(b).start()
        for e in range(RING):
            for c in weight_copies(e, e):
                c.start()
        xg[0, :, 0] = x_ref[...]
        g2 = scale_ref[0] * LOG2E
        phi_copy.wait()

        @pl.loop(0, n_slots // 512)
        def _(i):
            cols = pl.ds(pl.multiple_of(i * 512, 512), 512)
            v = phi[:, cols].astype(F32)
            phi[:, cols] = (v * lax.rsqrt(jnp.sum(v * v, axis=0, keepdims=True) + EPSILON)).astype(BF16)

        own = pl.ds(pl.multiple_of(s * (n_slots // 4) + d * slots, slots), slots)
        pnt[...] = phi[:, own].astype(F32).T.astype(BF16)

        @pl.loop(0, nb)
        def _(b):
            xn = unit_rows(x_ref[b].astype(F32))

            def chunk(i, carry):
                m, q = carry
                cols = pl.ds(pl.multiple_of(i * 512, 512), 512)
                lg = jnp.dot(xn, phi[:, cols], preferred_element_type=F32) * g2
                parts = [lg[:, 128 * k:128 * (k + 1)] for k in range(4)]
                m_new = jnp.maximum(m, jnp.maximum(jnp.maximum(parts[0], parts[1]), jnp.maximum(parts[2], parts[3])))
                e = [jnp.exp2(p - m_new) for p in parts]
                return m_new, q * jnp.exp2(m - m_new) + ((e[0] + e[1]) + (e[2] + e[3]))

            m, q = lax.fori_loop(0, n_slots // 512, chunk, (jnp.full((tok, 128), NEG_FILL, F32), jnp.zeros((tok, 128), F32)))
            big = jnp.max(m, axis=1, keepdims=True)
            tot = jnp.sum(q * jnp.exp2(m - big), axis=1, keepdims=True)
            pos = s * tok + lax.broadcasted_iota(jnp.int32, (1, tok), 1)
            rm[0, 0, pl.ds(b, 1), :] = row_of(big, tok)
            rm[0, 0, pl.ds(nb + b, 1), :] = jnp.where(pos < len_ref[b], 0.0, NEG_FILL)
            qrow[pl.ds(b, 1), :] = row_of(tot, tok)

        rm_x.start()
        rm_y.start()
        rm_p[0].start()

        def arrive(r, b):
            remote(xg.at[r, b, 0], xg.at[r, b, 0], sx_sem.at[0], r0_sem.at[4 * r + b], to_x).wait_recv()
            fwd_p(r, b).start()

        def unit(r, b, first):
            q = (r // 2) * nb + b
            remote(xg.at[r, b, 1], xg.at[r, b, 1], sp_sem.at[0], r1_sem.at[4 * r + b], to_p).wait_recv()
            xb = xg[r, b].reshape(2 * tok, dm)
            xn = unit_rows(xb.astype(F32))
            lt = lax.dot_general(pnt[...], xn, (((1,), (1,)), ((), ())), preferred_element_type=F32) * g2
            rmax = jnp.concatenate([rm[r, 0, pl.ds(b, 1), :], rm[r, 1, pl.ds(b, 1), :]], axis=1)
            mask = jnp.concatenate([rm[r, 0, pl.ds(nb + b, 1), :], rm[r, 1, pl.ds(nb + b, 1), :]], axis=1)
            ct[r, b] = jnp.exp2(lt - rmax).astype(BF16)
            lm = lt + mask
            mx = jnp.max(lm, axis=1, keepdims=True)
            if not first:
                m_old = m_s[q][:, 0:1]
                mx = jnp.maximum(mx, m_old)
            e = jnp.exp2(lm - mx)
            z = jnp.sum(e, axis=1, keepdims=True)
            part = jnp.dot(e.astype(BF16), xb, preferred_element_type=F32)
            if first:
                m_s[q] = jnp.broadcast_to(mx, (slots, 128))
                z_s[q] = jnp.broadcast_to(z, (slots, 128))
                acc[q] = part
            else:
                corr = jnp.exp2(m_old - mx)
                z = z + z_s[q][:, 0:1] * corr
                xs[q] = ((part + acc[q] * corr) / z).astype(BF16)

        remote(rm.at[0, 1], rm.at[0, 1], rms_sem.at[0], rm1_sem.at[0], to_p).wait_recv()

        @pl.loop(0, nb)
        def _(b):
            unit(0, b, True)

        for r, fwds in ((1, (rm_f, rm_p[1])), (2, (rm_p[2],))):
            remote(rm.at[r, 0], rm.at[r, 0], rms_sem.at[0], rm0_sem.at[r], to_x).wait_recv()
            for f in fwds:
                f.start()
        for r in (1, 2):
            remote(rm.at[r, 1], rm.at[r, 1], rms_sem.at[0], rm1_sem.at[r], to_p).wait_recv()

        @pl.loop(0, nb)
        def _(j):
            other = j + 1 - 2 * (j % 2)
            arrive(1, j)

            @pl.when(j % 2 == 0)
            def _():
                fwd_y(j).start()

            arrive(2, other)

            @pl.when(j % 2 == 0)
            def _():
                fwd_x(other).start()

            unit(1, j, False)
            unit(2, other, True)

        remote(rm.at[3, 0], rm.at[3, 0], rms_sem.at[0], rm0_sem.at[3], to_y).wait_recv()
        rm_p[3].start()
        remote(rm.at[3, 1], rm.at[3, 1], rms_sem.at[0], rm1_sem.at[3], to_p).wait_recv()

        @pl.loop(0, nb)
        def _(j):
            arrive(3, j)
            unit(3, j, False)

        for b in range(nb):
            send_x(b).wait_send()
            send_y(b).wait_send()
            send_p(b).wait_send()
            for r in (1, 2, 3):
                fwd_p(r, b).wait_send()
            (fwd_y(b) if b % 2 == 0 else fwd_x(b)).wait_send()
        for c in (rm_x, rm_y, rm_f, *rm_p):
            c.wait_send()

    pl.run_scoped(
        phase_dispatch,
        pltpu.VMEM((dm, n_slots), BF16),
        pltpu.VMEM((2 * nb, slots, dm), F32),
        pltpu.VMEM((2 * nb, slots, 128), F32),
        pltpu.VMEM((2 * nb, slots, 128), F32),
    )

    ff = w1b.shape[2]

    @pl.loop(0, n_exp)
    def _(e):
        slot = e % RING
        for c in weight_copies(e, slot):
            c.wait()
        rows = pl.ds(pl.multiple_of(e * 16, 16), 16)
        xe = xs[:, rows, :].reshape(2 * nb * 16, dm)
        total = jnp.zeros((2 * nb * 16, dm), F32)
        for k in range(0, ff, 512):
            h = jnp.dot(xe, w1b[slot, :, k:k + 512], preferred_element_type=F32)
            total += jnp.dot(gelu_tanh(h).astype(BF16), w2b[slot, k:k + 512, :], preferred_element_type=F32)
        xs[:, rows, :] = total.astype(BF16).reshape(2 * nb, 16, dm)

        @pl.when(e + RING < n_exp)
        def _():
            for c in weight_copies(e + RING, slot):
                c.start()

    def phase_combine(yst, d2s, stash):
        def d2_copy(r, b):
            return remote(d2s.at[r, b], d2r.at[r, b], d2s_sem.at[4 * r + b], d2r_sem.at[4 * r + b], to_p)

        def h_copy(b, odd):
            return remote(d2s.at[3, b], hr.at[b], hs_sem.at[b], hr_sem.at[b], to_y if odd else to_x)

        def f1_copy(b):
            return remote(d2s.at[1, b], f1r.at[b], f1s_sem.at[b], f1r_sem.at[b], to_x)

        def f2_copy(b):
            return remote(d2s.at[2, b], f2r.at[b], f2s_sem.at[b], f2r_sem.at[b], to_y)

        def comp(r, b, fresh):
            q = (r // 2) * nb + b
            if fresh:
                yst[q] = xs[q].astype(F32).T.astype(BF16)
            pt = jnp.dot(yst[q], ct[r, b], preferred_element_type=F32)
            d2s[r, b] = pt[:, tok:].astype(BF16)
            stash[r, b] = pt[:, :tok]
            d2_copy(r, b).start()

        def summed(r, b):
            d2_copy(r, b).wait()
            return stash[r, b] + d2r[r, b].astype(F32)

        @pl.loop(0, nb)
        def _(b):
            comp(3, b, True)

        @pl.loop(0, nb // 2)
        def _(j):
            b0, b1 = 2 * j, 2 * j + 1
            d2s[3, b0] = summed(3, b0).astype(BF16)
            h_copy(b0, False).start()
            d2s[3, b1] = summed(3, b1).astype(BF16)
            h_copy(b1, True).start()
            comp(1, b0, True)
            comp(2, b1, False)

        @pl.loop(0, nb // 2)
        def _(j):
            b0, b1 = 2 * j, 2 * j + 1
            d2s[1, b0] = summed(1, b0).astype(BF16)
            f1_copy(b0).start()
            d2s[2, b1] = summed(2, b1).astype(BF16)
            f2_copy(b1).start()
            comp(1, b1, True)
            comp(2, b0, False)

        @pl.loop(0, nb)
        def _(b):
            comp(0, b, False)

        @pl.loop(0, nb // 2)
        def _(j):
            b0, b1 = 2 * j, 2 * j + 1
            t1 = summed(1, b1)
            h_copy(b1, True).wait_recv()
            d2s[1, b1] = (t1 + hr[b1].astype(F32)).astype(BF16)
            f1_copy(b1).start()
            t2 = summed(2, b0)
            h_copy(b0, False).wait_recv()
            d2s[2, b0] = (t2 + hr[b0].astype(F32)).astype(BF16)
            f2_copy(b0).start()

        @pl.loop(0, nb)
        def _(b):
            t0 = summed(0, b)
            f1_copy(b).wait_recv()
            f2_copy(b).wait_recv()
            pos = s * tok + lax.broadcasted_iota(jnp.int32, (1, tok), 1)
            y = (t0 + f1r[b].astype(F32) + f2r[b].astype(F32)) / qrow[pl.ds(b, 1), :]
            y = jnp.where(pos < len_ref[b], y, 0.0)
            out_ref[b] = y.T.astype(BF16)

        for b in range(nb):
            h_copy(b, b % 2 == 1).wait_send()
            f1_copy(b).wait_send()
            f2_copy(b).wait_send()

    pl.run_scoped(
        phase_combine,
        pltpu.VMEM((2 * nb, dm, slots), BF16),
        pltpu.VMEM((4, nb, dm, tok), BF16),
        pltpu.VMEM((4, nb, dm, tok), F32),
    )


def solution(mesh):
    def local_layer(tok_blk, len_blk, slot_param, logit_scale, w_in, w_out):
        nb, tok, dm = tok_blk.shape
        n_slots = slot_param.shape[1]
        slots = n_slots // 8
        ff = w_in.shape[2]
        vmem = pl.BlockSpec(memory_space=pltpu.VMEM)
        smem = pl.BlockSpec(memory_space=pltpu.SMEM)
        hbm = pl.BlockSpec(memory_space=pl.ANY)
        dma = pltpu.SemaphoreType.DMA
        return pl.pallas_call(
            layer_kernel,
            out_shape=jax.ShapeDtypeStruct((nb, tok, dm), BF16),
            in_specs=[smem, smem, vmem, hbm, hbm, hbm],
            out_specs=vmem,
            scratch_shapes=[
                pltpu.VMEM((4, nb, 2, tok, dm), BF16),
                pltpu.VMEM((4, 2, 2 * nb, tok), F32),
                pltpu.VMEM((2 * nb, tok), F32),
                pltpu.VMEM((slots, dm), BF16),
                pltpu.VMEM((4, nb, slots, 2 * tok), BF16),
                pltpu.VMEM((2 * nb, slots, dm), BF16),
                pltpu.VMEM((4, nb, dm, tok), BF16),
                pltpu.VMEM((nb, dm, tok), BF16),
                pltpu.VMEM((nb, dm, tok), BF16),
                pltpu.VMEM((nb, dm, tok), BF16),
                pltpu.VMEM((RING, dm, ff), BF16),
                pltpu.VMEM((RING, ff, dm), BF16),
                dma((1,)), dma((RING,)), dma((RING,)),
                dma((nb,)), dma((nb,)), dma((4 * nb,)), dma((nb,)), dma((4 * nb,)), dma((4 * nb,)),
                dma((8,)), dma((4,)), dma((4,)),
                dma((4 * nb,)), dma((4 * nb,)), dma((nb,)), dma((nb,)), dma((nb,)), dma((nb,)), dma((nb,)), dma((nb,)),
            ],
            compiler_params=pltpu.CompilerParams(collective_id=0, has_side_effects=True, vmem_limit_bytes=67_000_000),
            name="soft_moe_layer",
        )(logit_scale.reshape(1), len_blk, tok_blk, slot_param, w_in, w_out)

    return jax.shard_map(local_layer, mesh=mesh, in_specs=(P("data", "seq", None), P("data"), P(None, None), P(), P("seq", None, None), P("seq", None, None)), out_specs=P("data", "seq", None), check_vma=False)
```

time: 353 us -> 120 us (0.34)
  waiting for transfers between devices: 214 us -> 0 us
  Pallas kernels: 0 us -> 117 us
  matrix products: 92.9 us -> 0 us
  other arithmetic: 21.1 us -> 0 us
  between operations: 13.9 us -> 0.66 us
  local copies, waits for them, and re-layouts: 10.9 us -> 2.09 us
    pallas_call x0 -> x1, Pallas kernels: none -> 117 us  [local_layer(): pl.pallas_call(layer_kernel, out_shape=jax.ShapeDtypeStruct((nb, tok, dm)...]
    dot_general x5 -> x0, matrix products: 92.9 us -> none  [the longest x1 31 us: local_layer(): jnp.einsum('besd,edf->besf', slot_grp, w_in, preferred_element_type=jnp.f...]
    reduce_scatter x1 -> x0, waiting for transfers between devices: 91.9 us -> none  [local_layer(): lax.psum_scatter(part_sum.astype(jnp.bfloat16), 'seq', scatter_dimension=...]
    all_gather x1 -> x0, waiting for transfers between devices: 80.1 us -> none  [local_layer(): lax.all_gather(own_out.reshape(batch_loc, slot_loc, d_model), 'seq', axis...]
    pmax x1 -> x0, waiting for transfers between devices: 28.9 us -> none  [local_layer(): col_max = lax.pmax(jnp.max(masked, axis=1, keepdims=True), 'seq')]
    reduce_sum x4 -> x0, other arithmetic: 18 us -> none  [the longest x1 8.75 us: local_layer(): jnp.sum(disp_w, axis=1)]
    unnamed x5 -> x0, waiting for transfers between devices: 12.9 us -> none
    unnamed x8 -> x1, local copies, waits for them, and re-layouts: 8.9 us -> 2.09 us
  transfers between devices with their start and end apart: 4 -> 0, of which waited for: 4 -> 0; matrix products, arithmetic and copies ran while one was open for 4% -> 0% of each run, Pallas kernels for 0% -> 0%
where the time goes in v1:
time: 120 us
  Pallas kernels  117 us (98%)
  local copies, waits for them, and re-layouts  2.09 us (2%)
    pallas_call x1, Pallas kernels, local_layer(): pl.pallas_call(layer_kernel, out_shape=jax.ShapeDtypeStruct((nb, tok, dm)...  117 us

profile of v1, /device:TPU:0, one launch (start us, length us, event | category | flops | bytes accessed | tf_op | source)
XLA Modules:
  0.0 119.5 jit_solution(8831015087453928660)
XLA Ops:
  0.7 116.8 %soft_moe_layer.1 = bf16[4,256,384]{2,1,0:T(8,128)(2,1)} custom-call(f32[1]{0:T(128)} %bitcast.1.scale_ref, s32[4]{0:T(128)} %len_ref.1, bf16[4,256,384]{2,1,0:T(8,128)(2,1)} %x_ref.1, bf16[384,4096]{1,0:T(8,128)(2,1)} %phi_hbm.1, bf16[64,384,1536]{2,1,0:T(8,128)(2,1)} %w1_hbm.1, bf16[64,1536,384]{2,1,0:T(8,128)(2,1)} %w2_hbm.1), custom_call_target="tpu_custom_call" | custom-call | tf_op jit(solution)/shard_map/soft_moe_layer/pallas_call | solution.py:345
  117.5 2.1 %copy.9 = bf16[4,256,384]{2,1,0:T(8,128)(2,1)} copy(bf16[4,256,384]{2,1,0:T(8,128)(2,1)} %soft_moe_layer.1) | data formatting | bytes 1572864

commit v2 on v1

--- a/solution.py
+++ b/solution.py
@@ -13,7 +13,7 @@
 LOG2E = 1.0 / math.log(2.0)
 F32 = jnp.float32
 BF16 = jnp.bfloat16
-RING = 7
+RING = 10
 
 
 def unit_rows(v32):
@@ -32,10 +32,10 @@
 
 def layer_kernel(
     scale_ref, len_ref, x_ref, phi_hbm, w1_hbm, w2_hbm, out_ref,
-    xg, rm, qrow, pnt, ct, xs, d2r, hr, f1r, f2r, w1b, w2b,
+    xg, rm, rqs, rqr, wrow, pnt, ct, xs, d2r, hr, f1r, f2r, w1b, w2b,
     phi_sem, w1_sem, w2_sem,
     sx_sem, sy_sem, sp_sem, sf_sem, r0_sem, r1_sem,
-    rms_sem, rm0_sem, rm1_sem,
+    rms_sem, rm0_sem, rm1_sem, rqs_sem, rqr_sem,
     d2s_sem, d2r_sem, hs_sem, hr_sem, f1s_sem, f1r_sem, f2s_sem, f2r_sem,
 ):
     nb, tok, dm = x_ref.shape
@@ -86,9 +86,16 @@
     rm_p = [remote(rm.at[r, 0], rm.at[r, 1], rms_sem.at[3 + r], rm1_sem.at[r], to_p) for r in range(4)]
 
     def phase_dispatch(phi, acc, m_s, z_s):
-        phi_copy = pltpu.make_async_copy(phi_hbm, phi, phi_sem.at[0])
+        own = pl.ds(pl.multiple_of(s * (n_slots // 4) + d * slots, slots), slots)
+        phi_copy = pltpu.make_async_copy(phi_hbm.at[:, own], phi, phi_sem.at[0])
         phi_copy.start()
+        pos = s * tok + lax.broadcasted_iota(jnp.int32, (1, tok), 1)
+        for b in range(nb):
+            rm[0, 0, b:b + 1, :] = jnp.where(pos < len_ref[b], 0.0, NEG_FILL)
         pl.semaphore_wait(barrier, 3)
+        rm_x.start()
+        rm_y.start()
+        rm_p[0].start()
         for b in range(nb):
             send_x(b).start()
             send_y(b ^ 1).start()
@@ -100,110 +107,90 @@
         xg[0, :, 0] = x_ref[...]
         g2 = scale_ref[0] * LOG2E
         phi_copy.wait()
-
-        @pl.loop(0, n_slots // 512)
-        def _(i):
-            cols = pl.ds(pl.multiple_of(i * 512, 512), 512)
-            v = phi[:, cols].astype(F32)
-            phi[:, cols] = (v * lax.rsqrt(jnp.sum(v * v, axis=0, keepdims=True) + EPSILON)).astype(BF16)
-
-        own = pl.ds(pl.multiple_of(s * (n_slots // 4) + d * slots, slots), slots)
-        pnt[...] = phi[:, own].astype(F32).T.astype(BF16)
-
-        @pl.loop(0, nb)
-        def _(b):
-            xn = unit_rows(x_ref[b].astype(F32))
-
-            def chunk(i, carry):
-                m, q = carry
-                cols = pl.ds(pl.multiple_of(i * 512, 512), 512)
-                lg = jnp.dot(xn, phi[:, cols], preferred_element_type=F32) * g2
-                parts = [lg[:, 128 * k:128 * (k + 1)] for k in range(4)]
-                m_new = jnp.maximum(m, jnp.maximum(jnp.maximum(parts[0], parts[1]), jnp.maximum(parts[2], parts[3])))
-                e = [jnp.exp2(p - m_new) for p in parts]
-                return m_new, q * jnp.exp2(m - m_new) + ((e[0] + e[1]) + (e[2] + e[3]))
-
-            m, q = lax.fori_loop(0, n_slots // 512, chunk, (jnp.full((tok, 128), NEG_FILL, F32), jnp.zeros((tok, 128), F32)))
-            big = jnp.max(m, axis=1, keepdims=True)
-            tot = jnp.sum(q * jnp.exp2(m - big), axis=1, keepdims=True)
-            pos = s * tok + lax.broadcasted_iota(jnp.int32, (1, tok), 1)
-            rm[0, 0, pl.ds(b, 1), :] = row_of(big, tok)
-            rm[0, 0, pl.ds(nb + b, 1), :] = jnp.where(pos < len_ref[b], 0.0, NEG_FILL)
-            qrow[pl.ds(b, 1), :] = row_of(tot, tok)
-
-        rm_x.start()
-        rm_y.start()
-        rm_p[0].start()
-
-        def arrive(r, b):
-            remote(xg.at[r, b, 0], xg.at[r, b, 0], sx_sem.at[0], r0_sem.at[4 * r + b], to_x).wait_recv()
-            fwd_p(r, b).start()
-
-        def unit(r, b, first):
-            q = (r // 2) * nb + b
-            remote(xg.at[r, b, 1], xg.at[r, b, 1], sp_sem.at[0], r1_sem.at[4 * r + b], to_p).wait_recv()
-            xb = xg[r, b].reshape(2 * tok, dm)
-            xn = unit_rows(xb.astype(F32))
-            lt = lax.dot_general(pnt[...], xn, (((1,), (1,)), ((), ())), preferred_element_type=F32) * g2
-            rmax = jnp.concatenate([rm[r, 0, pl.ds(b, 1), :], rm[r, 1, pl.ds(b, 1), :]], axis=1)
-            mask = jnp.concatenate([rm[r, 0, pl.ds(nb + b, 1), :], rm[r, 1, pl.ds(nb + b, 1), :]], axis=1)
-            ct[r, b] = jnp.exp2(lt - rmax).astype(BF16)
-            lm = lt + mask
-            mx = jnp.max(lm, axis=1, keepdims=True)
-            if not first:
-                m_old = m_s[q][:, 0:1]
-                mx = jnp.maximum(mx, m_old)
-            e = jnp.exp2(lm - mx)
-            z = jnp.sum(e, axis=1, keepdims=True)
-            part = jnp.dot(e.astype(BF16), xb, preferred_element_type=F32)
-            if first:
-                m_s[q] = jnp.broadcast_to(mx, (slots, 128))
-                z_s[q] = jnp.broadcast_to(z, (slots, 128))
-                acc[q] = part
-            else:
-                corr = jnp.exp2(m_old - mx)
-                z = z + z_s[q][:, 0:1] * corr
-                xs[q] = ((part + acc[q] * corr) / z).astype(BF16)
-
-        remote(rm.at[0, 1], rm.at[0, 1], rms_sem.at[0], rm1_sem.at[0], to_p).wait_recv()
-
-        @pl.loop(0, nb)
-        def _(b):
-            unit(0, b, True)
-
+        v = phi[...].astype(F32)
+        pnt[...] = (v * lax.rsqrt(jnp.sum(v * v, axis=0, keepdims=True) + EPSILON)).T.astype(BF16)
         for r, fwds in ((1, (rm_f, rm_p[1])), (2, (rm_p[2],))):
             remote(rm.at[r, 0], rm.at[r, 0], rms_sem.at[0], rm0_sem.at[r], to_x).wait_recv()
             for f in fwds:
                 f.start()
+
+        def arrive(r, b):
+            remote(xg.at[r, b, 0], xg.at[r, b, 0], sx_sem.at[0], r0_sem.at[4 * r + b], to_x).wait_recv()
+            fwd_p(r, b).start()
+
+        def wait_partner(r, b):
+            remote(xg.at[r, b, 1], xg.at[r, b, 1], sp_sem.at[0], r1_sem.at[4 * r + b], to_p).wait_recv()
+
+        def wait_mask(r):
+            remote(rm.at[r, 1], rm.at[r, 1], rms_sem.at[0], rm1_sem.at[r], to_p).wait_recv()
+
+        def unit(r, b, first):
+            q = (r // 2) * nb + b
+            xb = xg[r, b].reshape(2 * tok, dm)
+            xn = unit_rows(xb.astype(F32))
+            lt = lax.dot_general(pnt[...], xn, (((1,), (1,)), ((), ())), preferred_element_type=F32) * g2
+            mask = jnp.concatenate([rm[r, 0, pl.ds(b, 1), :], rm[r, 1, pl.ds(b, 1), :]], axis=1)
+            lm = lt + mask
+            mx = jnp.broadcast_to(jnp.max(lm, axis=1, keepdims=True), (slots, 128))
+            if not first:
+                m_old = m_s[q]
+                mx = jnp.maximum(mx, m_old)
+            e = jnp.exp2(lm - jnp.concatenate([mx] * 4, axis=1))
+            z = (e[:, 0:128] + e[:, 128:256]) + (e[:, 256:384] + e[:, 384:512])
+            part = jnp.dot(e.astype(BF16), xb, preferred_element_type=F32)
+            cmax = jnp.max(lt, axis=0, keepdims=True)
+            c = jnp.exp2(lt - cmax)
+            rqs[0, r, pl.ds(b, 1), :] = cmax
+            rqs[0, r, pl.ds(nb + b, 1), :] = jnp.sum(c, axis=0, keepdims=True)
+            ct[r, b] = c.astype(BF16)
+            if first:
+                m_s[q] = mx
+                z_s[q] = z
+                acc[q] = part
+            else:
+                corr = jnp.exp2(m_old - mx)
+                z = jnp.broadcast_to(jnp.sum(z + z_s[q] * corr, axis=1, keepdims=True), (slots, 128))
+                inv = 1.0 / z
+                xs[q] = ((part + acc[q] * jnp.concatenate([corr] * 3, axis=1)) * jnp.concatenate([inv] * 3, axis=1)).astype(BF16)
+
+        wait_mask(0)
+
+        @pl.loop(0, nb)
+        def _(b):
+            wait_partner(0, b)
+            unit(0, b, True)
+
         for r in (1, 2):
-            remote(rm.at[r, 1], rm.at[r, 1], rms_sem.at[0], rm1_sem.at[r], to_p).wait_recv()
+            wait_mask(r)
 
         @pl.loop(0, nb)
         def _(j):
             other = j + 1 - 2 * (j % 2)
             arrive(1, j)
+            arrive(2, other)
 
             @pl.when(j % 2 == 0)
             def _():
                 fwd_y(j).start()
-
-            arrive(2, other)
-
-            @pl.when(j % 2 == 0)
-            def _():
                 fwd_x(other).start()
 
+            wait_partner(1, j)
+            wait_partner(2, other)
             unit(1, j, False)
             unit(2, other, True)
 
         remote(rm.at[3, 0], rm.at[3, 0], rms_sem.at[0], rm0_sem.at[3], to_y).wait_recv()
         rm_p[3].start()
-        remote(rm.at[3, 1], rm.at[3, 1], rms_sem.at[0], rm1_sem.at[3], to_p).wait_recv()
-
-        @pl.loop(0, nb)
-        def _(j):
-            arrive(3, j)
-            unit(3, j, False)
+        wait_mask(3)
+
+        @pl.loop(0, nb // 2)
+        def _(j):
+            for b in (2 * j, 2 * j + 1):
+                arrive(3, b)
+            for b in (2 * j, 2 * j + 1):
+                wait_partner(3, b)
+            for b in (2 * j, 2 * j + 1):
+                unit(3, b, False)
 
         for b in range(nb):
             send_x(b).wait_send()
@@ -217,31 +204,57 @@
 
     pl.run_scoped(
         phase_dispatch,
-        pltpu.VMEM((dm, n_slots), BF16),
+        pltpu.VMEM((dm, slots), BF16),
         pltpu.VMEM((2 * nb, slots, dm), F32),
         pltpu.VMEM((2 * nb, slots, 128), F32),
         pltpu.VMEM((2 * nb, slots, 128), F32),
     )
 
-    ff = w1b.shape[2]
-
-    @pl.loop(0, n_exp)
-    def _(e):
-        slot = e % RING
-        for c in weight_copies(e, slot):
-            c.wait()
-        rows = pl.ds(pl.multiple_of(e * 16, 16), 16)
-        xe = xs[:, rows, :].reshape(2 * nb * 16, dm)
-        total = jnp.zeros((2 * nb * 16, dm), F32)
-        for k in range(0, ff, 512):
-            h = jnp.dot(xe, w1b[slot, :, k:k + 512], preferred_element_type=F32)
-            total += jnp.dot(gelu_tanh(h).astype(BF16), w2b[slot, k:k + 512, :], preferred_element_type=F32)
-        xs[:, rows, :] = total.astype(BF16).reshape(2 * nb, 16, dm)
-
-        @pl.when(e + RING < n_exp)
-        def _():
-            for c in weight_copies(e + RING, slot):
-                c.start()
+    rq_copies = [remote(rqs.at[k], rqr.at[k], rqs_sem.at[k], rqr_sem.at[k], dev) for k, dev in enumerate((to_p, to_x, to_y))]
+
+    def merge(k):
+        rq_copies[k].wait()
+        for r in range(4):
+            if k == 0:
+                theirs = jnp.concatenate([rqr[k, r][:, tok:], rqr[k, r][:, :tok]], axis=1)
+            else:
+                theirs = rqr[k, r ^ k]
+            mine = rqs[k, r]
+            top = jnp.maximum(mine[:nb], theirs[:nb])
+            low = mine[nb:] * jnp.exp2(mine[:nb] - top) + theirs[nb:] * jnp.exp2(theirs[:nb] - top)
+            rqs[k + 1, r, :nb] = top
+            rqs[k + 1, r, nb:] = low
+            if k == 2:
+                wrow[r] = jnp.exp2(rqs[0, r][:nb] - top)
+        if k < 2:
+            rq_copies[k + 1].start()
+
+    rq_copies[0].start()
+
+    def ffn_pair(i):
+        pair = (2 * i, 2 * i + 1)
+        for e in pair:
+            for c in weight_copies(e, e % RING):
+                c.wait()
+        rows = [pl.ds(pl.multiple_of(e * 16, 16), 16) for e in pair]
+        xe = [xs[:, r, :].reshape(2 * nb * 16, dm) for r in rows]
+        hs = [jnp.dot(x, w1b[e % RING], preferred_element_type=F32) for x, e in zip(xe, pair)]
+        ys = [jnp.dot(gelu_tanh(h).astype(BF16), w2b[e % RING], preferred_element_type=F32) for h, e in zip(hs, pair)]
+        for y, r in zip(ys, rows):
+            xs[:, r, :] = y.astype(BF16).reshape(2 * nb, 16, dm)
+        for e in pair:
+            @pl.when(e + RING < n_exp)
+            def _():
+                for c in weight_copies(e + RING, e % RING):
+                    c.start()
+
+    @pl.loop(0, n_exp // 2)
+    def _(i):
+        ffn_pair(i)
+        for k in range(3):
+            @pl.when(i == 4 * (k + 1))
+            def _():
+                merge(k)
 
     def phase_combine(yst, d2s, stash):
         def d2_copy(r, b):
@@ -261,6 +274,7 @@
             if fresh:
                 yst[q] = xs[q].astype(F32).T.astype(BF16)
             pt = jnp.dot(yst[q], ct[r, b], preferred_element_type=F32)
+            pt = pt * wrow[r, pl.ds(b, 1), :]
             d2s[r, b] = pt[:, tok:].astype(BF16)
             stash[r, b] = pt[:, :tok]
             d2_copy(r, b).start()
@@ -315,7 +329,7 @@
             f1_copy(b).wait_recv()
             f2_copy(b).wait_recv()
             pos = s * tok + lax.broadcasted_iota(jnp.int32, (1, tok), 1)
-            y = (t0 + f1r[b].astype(F32) + f2r[b].astype(F32)) / qrow[pl.ds(b, 1), :]
+            y = (t0 + f1r[b].astype(F32) + f2r[b].astype(F32)) / rqs[3, 0, pl.ds(nb + b, 1), :tok]
             y = jnp.where(pos < len_ref[b], y, 0.0)
             out_ref[b] = y.T.astype(BF16)
 
@@ -349,8 +363,10 @@
             out_specs=vmem,
             scratch_shapes=[
                 pltpu.VMEM((4, nb, 2, tok, dm), BF16),
-                pltpu.VMEM((4, 2, 2 * nb, tok), F32),
-                pltpu.VMEM((2 * nb, tok), F32),
+                pltpu.VMEM((4, 2, nb, tok), F32),
+                pltpu.VMEM((4, 4, 2 * nb, 2 * tok), F32),
+                pltpu.VMEM((3, 4, 2 * nb, 2 * tok), F32),
+                pltpu.VMEM((4, nb, 2 * tok), F32),
                 pltpu.VMEM((slots, dm), BF16),
                 pltpu.VMEM((4, nb, slots, 2 * tok), BF16),
                 pltpu.VMEM((2 * nb, slots, dm), BF16),
@@ -362,7 +378,7 @@
                 pltpu.VMEM((RING, ff, dm), BF16),
                 dma((1,)), dma((RING,)), dma((RING,)),
                 dma((nb,)), dma((nb,)), dma((4 * nb,)), dma((nb,)), dma((4 * nb,)), dma((4 * nb,)),
-                dma((8,)), dma((4,)), dma((4,)),
+                dma((8,)), dma((4,)), dma((4,)), dma((3,)), dma((3,)),
                 dma((4 * nb,)), dma((4 * nb,)), dma((nb,)), dma((nb,)), dma((nb,)), dma((nb,)), dma((nb,)), dma((nb,)),
             ],
             compiler_params=pltpu.CompilerParams(collective_id=0, has_side_effects=True, vmem_limit_bytes=67_000_000),

time: 120 us -> 89.2 us (0.74)
  Pallas kernels: 117 us -> 86.3 us
    pallas_call x1, Pallas kernels: 117 us -> 86.3 us  [local_layer(): pl.pallas_call(layer_kernel, out_shape=jax.ShapeDtypeStruct((nb, tok, dm)...]
where the time goes in v2:
time: 89.2 us; the launch traced here: 89.1 us
  Pallas kernels  86.3 us (97%)
  local copies, waits for them, and re-layouts  2.09 us (2%)
    pallas_call x1, Pallas kernels, local_layer(): pl.pallas_call(layer_kernel, out_shape=jax.ShapeDtypeStruct((nb, tok, dm)...  86.3 us
    unnamed x1, local copies, waits for them, and re-layouts  2.09 us

profile of v2, /device:TPU:0, one launch (start us, length us, event | category | flops | bytes accessed | tf_op | source)
XLA Modules:
  0.0 89.1 jit_solution(16087798513312076939)
XLA Ops:
  0.7 86.3 %soft_moe_layer.1 = bf16[4,256,384]{2,1,0:T(8,128)(2,1)} custom-call(f32[1]{0:T(128)} %bitcast.1.scale_ref, s32[4]{0:T(128)} %len_ref.1, bf16[4,256,384]{2,1,0:T(8,128)(2,1)} %x_ref.1, bf16[384,4096]{1,0:T(8,128)(2,1)} %phi_hbm.1, bf16[64,384,1536]{2,1,0:T(8,128)(2,1)} %w1_hbm.1, bf16[64,1536,384]{2,1,0:T(8,128)(2,1)} %w2_hbm.1), custom_call_target="tpu_custom_call" | custom-call | tf_op jit(solution)/shard_map/soft_moe_layer/pallas_call | solution.py:359
  87.0 2.1 %copy.9 = bf16[4,256,384]{2,1,0:T(8,128)(2,1)} copy(bf16[4,256,384]{2,1,0:T(8,128)(2,1)} %soft_moe_layer.1) | data formatting | bytes 1572864
